TPU v7x, 64 devices: a 2x2x8 block of a 4x4x8 slice. The times are simulated.
64 devices in a mesh: dp: 4 (over x, y), sp: 16 (over z, core).
Axes of the slice: x: 2, y: 2, z: 8, core: 2. Of those that a mesh axis runs over, the one named last changes fastest.
The devices are a block of a 4x4x8 slice.
Arguments:
- z_points: bfloat16 [131072, 512], P(('dp', 'sp')), parts along dimension 0
- x_points: bfloat16 [32768, 512], P(('dp', 'sp')), parts along dimension 0
- rhs_vals: bfloat16 [32768, 32], P(('dp', 'sp')), parts along dimension 0
- block_mask: int32 [64, 16], P(('dp', 'sp')), parts along dimension 0
- length_scale: float32 [1], replicated
- out_scale: float32 [1], replicated
Outputs:
- output: float32 [131072, 32], P(('dp', 'sp')), parts along dimension 0
There are 4 independent parts. A program takes and returns all parts, laid end to end along the dimension named above; an argument that names none is the same for every part.
All inputs are finite; a program needn't handle non-finite values.
Results may differ from a plain program's by a relative error of at most 0.001.
Values are sent between devices in bfloat16 or wider.
A program may use at most 768 MiB of HBM per device.

v0:
```python
import jax
import jax.numpy as jnp
from jax import lax
from jax.sharding import PartitionSpec as P


def block_product(z_rows, z_norm, x_rows, v_rows, ell_sq, scale_val):
    x_norm = jnp.einsum("nd,nd->n", x_rows, x_rows, preferred_element_type=jnp.float32)
    gram_blk = jnp.einsum("md,nd->mn", z_rows, x_rows, preferred_element_type=jnp.float32)
    sq_dist = jnp.maximum(z_norm[:, None] + x_norm[None, :] - 2.0 * gram_blk, 0.0)
    kern_blk = (scale_val * jnp.exp(-sq_dist / (2.0 * ell_sq))).astype(jnp.bfloat16)
    return jnp.dot(kern_blk, v_rows, preferred_element_type=jnp.float32)


def solution(mesh):
    group_size = mesh.shape["sp"]
    shift_pairs = [(dev_idx, (dev_idx + 1) % group_size) for dev_idx in range(group_size)]
    row_spec = P(("dp", "sp"), None)

    def local_fn(z_rows, x_rows, v_rows, mask_row, length_scale, out_scale):
        my_index = lax.axis_index("sp")
        ell_sq = length_scale[0] * length_scale[0]
        scale_val = out_scale[0]
        weights = mask_row[0].astype(jnp.float32)
        z_norm = jnp.einsum("md,md->m", z_rows, z_rows, preferred_element_type=jnp.float32)
        first_y = block_product(z_rows, z_norm, x_rows, v_rows, ell_sq, scale_val) * weights[my_index]

        def shift_step(step_idx, loop_state):
            x_cur, v_cur, y_acc = loop_state
            x_cur = lax.ppermute(x_cur, "sp", shift_pairs)
            v_cur = lax.ppermute(v_cur, "sp", shift_pairs)
            src_block = (my_index - step_idx) % group_size
            part_y = block_product(z_rows, z_norm, x_cur, v_cur, ell_sq, scale_val)
            return (x_cur, v_cur, y_acc + part_y * weights[src_block])

        final_state = lax.fori_loop(1, group_size, shift_step, (x_rows, v_rows, first_y))
        return final_state[2]

    return jax.shard_map(local_fn, mesh=mesh, in_specs=(row_spec, row_spec, row_spec, row_spec, P(None), P(None)), out_specs=row_spec, check_vma=False)
```

profile of v0, /device:TPU:22, one launch (start us, length us, event | category | flops | bytes accessed | tf_op | source)
XLA Modules:
  0.0 227.3 jit_solution(10121619383247785517)
XLA Ops:
  9.9 216.7 %while.19 = (s32[]{:T(128)}, bf16[512,512]{1,0:T(8,128)(2,1)S(1)}, bf16[512,32]{0,1:T(8,128)(2,1)S(1)}, f32[2048,32]{0,1:T(8,128)S(1)}, f32[]{:T(128)}, /*index=...) while((s32[]{:T(128)}, bf16[512,512]{1,0:T(8,128)(2,1)S(1)}, ...), condition=%wide.region_1.2_spmd, body=%wide.region_0.1_spmd.sunk | while | flops 1150156288 | bytes 7057800 | solution.py:36
  12.8 11.2 %collective-permute-done.1 = bf16[512,32]{0,1:T(8,128)(2,1)S(1)} collective-permute-done((bf16[512,32]{0,1:T(8,128)(2,1)S(1)}, bf16[512,32]{0,1:T(8,128)(2,1)S(1)}, u32[]{:S(2)}, u32[]{:S(2)}) %collective-permute-start.1) | collective-permute-done | bytes 32800 | tf_op jit(solution)/shard_map/while/body/eval_jaxpr/ppermute | solution.py:31
  24.2 3.7 %fusion.23 = f32[2048,32]{0,1:T(8,128)S(1)} fusion(f32[2048,32]{0,1:T(8,128)S(1)} %get-tuple-element.351, bf16[512,32]{0,1:T(8,128)(2,1)S(1)} %collective-permute-done.1, bf16[2048,512]{1,0:T(8,128)(2,1)S(1)} %get-tuple-element.368, bf16[512,512]{1,0:T(8,128)(2,1)S(1)} %collective-permute-done, f32[]{:T(128)} %get-tuple-element.369, ...), kind=kOutput, calls=%fused_computation.2.clone.1 | convolution fusion | flops 1149370368 | bytes 3188748 | tf_op jit(solution)/shard_map/while/body/eval_jaxpr/dot_general | solution.py:12
  28.7 9.4 %collective-permute-done.1 = bf16[512,32]{0,1:T(8,128)(2,1)S(1)} collective-permute-done((bf16[512,32]{0,1:T(8,128)(2,1)S(1)}, bf16[512,32]{0,1:T(8,128)(2,1)S(1)}, u32[]{:S(2)}, u32[]{:S(2)}) %collective-permute-start.1) | collective-permute-done | bytes 32800 | tf_op jit(solution)/shard_map/while/body/eval_jaxpr/ppermute | solution.py:31
  38.4 3.7 %fusion.23 = f32[2048,32]{0,1:T(8,128)S(1)} fusion(f32[2048,32]{0,1:T(8,128)S(1)} %get-tuple-element.351, bf16[512,32]{0,1:T(8,128)(2,1)S(1)} %collective-permute-done.1, bf16[2048,512]{1,0:T(8,128)(2,1)S(1)} %get-tuple-element.368, bf16[512,512]{1,0:T(8,128)(2,1)S(1)} %collective-permute-done, f32[]{:T(128)} %get-tuple-element.369, ...), kind=kOutput, calls=%fused_computation.2.clone.1 | convolution fusion | flops 1149370368 | bytes 3188748 | tf_op jit(solution)/shard_map/while/body/eval_jaxpr/dot_general | solution.py:12
  42.9 9.4 %collective-permute-done.1 = bf16[512,32]{0,1:T(8,128)(2,1)S(1)} collective-permute-done((bf16[512,32]{0,1:T(8,128)(2,1)S(1)}, bf16[512,32]{0,1:T(8,128)(2,1)S(1)}, u32[]{:S(2)}, u32[]{:S(2)}) %collective-permute-start.1) | collective-permute-done | bytes 32800 | tf_op jit(solution)/shard_map/while/body/eval_jaxpr/ppermute | solution.py:31
  52.5 3.7 %fusion.23 = f32[2048,32]{0,1:T(8,128)S(1)} fusion(f32[2048,32]{0,1:T(8,128)S(1)} %get-tuple-element.351, bf16[512,32]{0,1:T(8,128)(2,1)S(1)} %collective-permute-done.1, bf16[2048,512]{1,0:T(8,128)(2,1)S(1)} %get-tuple-element.368, bf16[512,512]{1,0:T(8,128)(2,1)S(1)} %collective-permute-done, f32[]{:T(128)} %get-tuple-element.369, ...), kind=kOutput, calls=%fused_computation.2.clone.1 | convolution fusion | flops 1149370368 | bytes 3188748 | tf_op jit(solution)/shard_map/while/body/eval_jaxpr/dot_general | solution.py:12
  57.1 9.4 %collective-permute-done.1 = bf16[512,32]{0,1:T(8,128)(2,1)S(1)} collective-permute-done((bf16[512,32]{0,1:T(8,128)(2,1)S(1)}, bf16[512,32]{0,1:T(8,128)(2,1)S(1)}, u32[]{:S(2)}, u32[]{:S(2)}) %collective-permute-start.1) | collective-permute-done | bytes 32800 | tf_op jit(solution)/shard_map/while/body/eval_jaxpr/ppermute | solution.py:31
  66.7 3.7 %fusion.23 = f32[2048,32]{0,1:T(8,128)S(1)} fusion(f32[2048,32]{0,1:T(8,128)S(1)} %get-tuple-element.351, bf16[512,32]{0,1:T(8,128)(2,1)S(1)} %collective-permute-done.1, bf16[2048,512]{1,0:T(8,128)(2,1)S(1)} %get-tuple-element.368, bf16[512,512]{1,0:T(8,128)(2,1)S(1)} %collective-permute-done, f32[]{:T(128)} %get-tuple-element.369, ...), kind=kOutput, calls=%fused_computation.2.clone.1 | convolution fusion | flops 1149370368 | bytes 3188748 | tf_op jit(solution)/shard_map/while/body/eval_jaxpr/dot_general | solution.py:12
  71.3 9.4 %collective-permute-done.1 = bf16[512,32]{0,1:T(8,128)(2,1)S(1)} collective-permute-done((bf16[512,32]{0,1:T(8,128)(2,1)S(1)}, bf16[512,32]{0,1:T(8,128)(2,1)S(1)}, u32[]{:S(2)}, u32[]{:S(2)}) %collective-permute-start.1) | collective-permute-done | bytes 32800 | tf_op jit(solution)/shard_map/while/body/eval_jaxpr/ppermute | solution.py:31
  85.5 9.4 %collective-permute-done.1 = bf16[512,32]{0,1:T(8,128)(2,1)S(1)} collective-permute-done((bf16[512,32]{0,1:T(8,128)(2,1)S(1)}, bf16[512,32]{0,1:T(8,128)(2,1)S(1)}, u32[]{:S(2)}, u32[]{:S(2)}) %collective-permute-start.1) | collective-permute-done | bytes 32800 | tf_op jit(solution)/shard_map/while/body/eval_jaxpr/ppermute | solution.py:31
  95.1 3.7 %fusion.23 = f32[2048,32]{0,1:T(8,128)S(1)} fusion(f32[2048,32]{0,1:T(8,128)S(1)} %get-tuple-element.351, bf16[512,32]{0,1:T(8,128)(2,1)S(1)} %collective-permute-done.1, bf16[2048,512]{1,0:T(8,128)(2,1)S(1)} %get-tuple-element.368, bf16[512,512]{1,0:T(8,128)(2,1)S(1)} %collective-permute-done, f32[]{:T(128)} %get-tuple-element.369, ...), kind=kOutput, calls=%fused_computation.2.clone.1 | convolution fusion | flops 1149370368 | bytes 3188748 | tf_op jit(solution)/shard_map/while/body/eval_jaxpr/dot_general | solution.py:12
  99.6 9.4 %collective-permute-done.1 = bf16[512,32]{0,1:T(8,128)(2,1)S(1)} collective-permute-done((bf16[512,32]{0,1:T(8,128)(2,1)S(1)}, bf16[512,32]{0,1:T(8,128)(2,1)S(1)}, u32[]{:S(2)}, u32[]{:S(2)}) %collective-permute-start.1) | collective-permute-done | bytes 32800 | tf_op jit(solution)/shard_map/while/body/eval_jaxpr/ppermute | solution.py:31
  113.8 9.4 %collective-permute-done.1 = bf16[512,32]{0,1:T(8,128)(2,1)S(1)} collective-permute-done((bf16[512,32]{0,1:T(8,128)(2,1)S(1)}, bf16[512,32]{0,1:T(8,128)(2,1)S(1)}, u32[]{:S(2)}, u32[]{:S(2)}) %collective-permute-start.1) | collective-permute-done | bytes 32800 | tf_op jit(solution)/shard_map/while/body/eval_jaxpr/ppermute | solution.py:31
  128.0 9.4 %collective-permute-done.1 = bf16[512,32]{0,1:T(8,128)(2,1)S(1)} collective-permute-done((bf16[512,32]{0,1:T(8,128)(2,1)S(1)}, bf16[512,32]{0,1:T(8,128)(2,1)S(1)}, u32[]{:S(2)}, u32[]{:S(2)}) %collective-permute-start.1) | collective-permute-done | bytes 32800 | tf_op jit(solution)/shard_map/while/body/eval_jaxpr/ppermute | solution.py:31
  137.7 3.7 %fusion.23 = f32[2048,32]{0,1:T(8,128)S(1)} fusion(f32[2048,32]{0,1:T(8,128)S(1)} %get-tuple-element.351, bf16[512,32]{0,1:T(8,128)(2,1)S(1)} %collective-permute-done.1, bf16[2048,512]{1,0:T(8,128)(2,1)S(1)} %get-tuple-element.368, bf16[512,512]{1,0:T(8,128)(2,1)S(1)} %collective-permute-done, f32[]{:T(128)} %get-tuple-element.369, ...), kind=kOutput, calls=%fused_computation.2.clone.1 | convolution fusion | flops 1149370368 | bytes 3188748 | tf_op jit(solution)/shard_map/while/body/eval_jaxpr/dot_general | solution.py:12
  142.2 9.4 %collective-permute-done.1 = bf16[512,32]{0,1:T(8,128)(2,1)S(1)} collective-permute-done((bf16[512,32]{0,1:T(8,128)(2,1)S(1)}, bf16[512,32]{0,1:T(8,128)(2,1)S(1)}, u32[]{:S(2)}, u32[]{:S(2)}) %collective-permute-start.1) | collective-permute-done | bytes 32800 | tf_op jit(solution)/shard_map/while/body/eval_jaxpr/ppermute | solution.py:31
  156.4 9.4 %collective-permute-done.1 = bf16[512,32]{0,1:T(8,128)(2,1)S(1)} collective-permute-done((bf16[512,32]{0,1:T(8,128)(2,1)S(1)}, bf16[512,32]{0,1:T(8,128)(2,1)S(1)}, u32[]{:S(2)}, u32[]{:S(2)}) %collective-permute-start.1) | collective-permute-done | bytes 32800 | tf_op jit(solution)/shard_map/while/body/eval_jaxpr/ppermute | solution.py:31
  170.6 9.4 %collective-permute-done.1 = bf16[512,32]{0,1:T(8,128)(2,1)S(1)} collective-permute-done((bf16[512,32]{0,1:T(8,128)(2,1)S(1)}, bf16[512,32]{0,1:T(8,128)(2,1)S(1)}, u32[]{:S(2)}, u32[]{:S(2)}) %collective-permute-start.1) | collective-permute-done | bytes 32800 | tf_op jit(solution)/shard_map/while/body/eval_jaxpr/ppermute | solution.py:31
  180.3 3.7 %fusion.23 = f32[2048,32]{0,1:T(8,128)S(1)} fusion(f32[2048,32]{0,1:T(8,128)S(1)} %get-tuple-element.351, bf16[512,32]{0,1:T(8,128)(2,1)S(1)} %collective-permute-done.1, bf16[2048,512]{1,0:T(8,128)(2,1)S(1)} %get-tuple-element.368, bf16[512,512]{1,0:T(8,128)(2,1)S(1)} %collective-permute-done, f32[]{:T(128)} %get-tuple-element.369, ...), kind=kOutput, calls=%fused_computation.2.clone.1 | convolution fusion | flops 1149370368 | bytes 3188748 | tf_op jit(solution)/shard_map/while/body/eval_jaxpr/dot_general | solution.py:12
  184.8 9.4 %collective-permute-done.1 = bf16[512,32]{0,1:T(8,128)(2,1)S(1)} collective-permute-done((bf16[512,32]{0,1:T(8,128)(2,1)S(1)}, bf16[512,32]{0,1:T(8,128)(2,1)S(1)}, u32[]{:S(2)}, u32[]{:S(2)}) %collective-permute-start.1) | collective-permute-done | bytes 32800 | tf_op jit(solution)/shard_map/while/body/eval_jaxpr/ppermute | solution.py:31
  199.0 9.4 %collective-permute-done.1 = bf16[512,32]{0,1:T(8,128)(2,1)S(1)} collective-permute-done((bf16[512,32]{0,1:T(8,128)(2,1)S(1)}, bf16[512,32]{0,1:T(8,128)(2,1)S(1)}, u32[]{:S(2)}, u32[]{:S(2)}) %collective-permute-start.1) | collective-permute-done | bytes 32800 | tf_op jit(solution)/shard_map/while/body/eval_jaxpr/ppermute | solution.py:31
  213.2 9.4 %collective-permute-done.1 = bf16[512,32]{0,1:T(8,128)(2,1)S(1)} collective-permute-done((bf16[512,32]{0,1:T(8,128)(2,1)S(1)}, bf16[512,32]{0,1:T(8,128)(2,1)S(1)}, u32[]{:S(2)}, u32[]{:S(2)}) %collective-permute-start.1) | collective-permute-done | bytes 32800 | tf_op jit(solution)/shard_map/while/body/eval_jaxpr/ppermute | solution.py:31
  222.8 3.7 %fusion.23 = f32[2048,32]{0,1:T(8,128)S(1)} fusion(f32[2048,32]{0,1:T(8,128)S(1)} %get-tuple-element.351, bf16[512,32]{0,1:T(8,128)(2,1)S(1)} %collective-permute-done.1, bf16[2048,512]{1,0:T(8,128)(2,1)S(1)} %get-tuple-element.368, bf16[512,512]{1,0:T(8,128)(2,1)S(1)} %collective-permute-done, f32[]{:T(128)} %get-tuple-element.369, ...), kind=kOutput, calls=%fused_computation.2.clone.1 | convolution fusion | flops 1149370368 | bytes 3188748 | tf_op jit(solution)/shard_map/while/body/eval_jaxpr/dot_general | solution.py:12
  (123 shorter events, 51.9 us)
Async XLA Ops:
  9.9 14.1 %collective-permute-start = (bf16[512,512]{1,0:T(8,128)(2,1)S(1)}, bf16[512,512]{1,0:T(8,128)(2,1)S(1)}, u32[]{:S(2)}, u32[]{:S(2)}) collective-permute-start(bf16[512,512]{1,0:T(8,128)(2,1)S(1)} %get-tuple-element.349), channel_id=1, source_target_pairs={{0,1},{1,2},{2,3},{3,4},{4,5},{5,6},{6,7},{7,8},{8,9},{9,10},{10,1... | collective-permute-start | bytes 1572872 | tf_op jit(solution)/shard_map/while/body/eval_jaxpr/ppermute | solution.py:30
  10.0 14.0 %collective-permute-start.1 = (bf16[512,32]{0,1:T(8,128)(2,1)S(1)}, bf16[512,32]{0,1:T(8,128)(2,1)S(1)}, u32[]{:S(2)}, u32[]{:S(2)}) collective-permute-start(bf16[512,32]{0,1:T(8,128)(2,1)S(1)} %get-tuple-element.350), channel_id=1, source_target_pairs={{0,1},{1,2},{2,3},{3,4},{4,5},{5,6},{6,7},{7,8},{8,9},{9,10},{10,1... | collective-permute-start | bytes 98312 | tf_op jit(solution)/shard_map/while/body/eval_jaxpr/ppermute | solution.py:31
  27.9 10.2 %collective-permute-start = (bf16[512,512]{1,0:T(8,128)(2,1)S(1)}, bf16[512,512]{1,0:T(8,128)(2,1)S(1)}, u32[]{:S(2)}, u32[]{:S(2)}) collective-permute-start(bf16[512,512]{1,0:T(8,128)(2,1)S(1)} %get-tuple-element.349), channel_id=1, source_target_pairs={{0,1},{1,2},{2,3},{3,4},{4,5},{5,6},{6,7},{7,8},{8,9},{9,10},{10,1... | collective-permute-start | bytes 1572872 | tf_op jit(solution)/shard_map/while/body/eval_jaxpr/ppermute | solution.py:30
  28.0 10.1 %collective-permute-start.1 = (bf16[512,32]{0,1:T(8,128)(2,1)S(1)}, bf16[512,32]{0,1:T(8,128)(2,1)S(1)}, u32[]{:S(2)}, u32[]{:S(2)}) collective-permute-start(bf16[512,32]{0,1:T(8,128)(2,1)S(1)} %get-tuple-element.350), channel_id=1, source_target_pairs={{0,1},{1,2},{2,3},{3,4},{4,5},{5,6},{6,7},{7,8},{8,9},{9,10},{10,1... | collective-permute-start | bytes 98312 | tf_op jit(solution)/shard_map/while/body/eval_jaxpr/ppermute | solution.py:31
  42.1 10.2 %collective-permute-start = (bf16[512,512]{1,0:T(8,128)(2,1)S(1)}, bf16[512,512]{1,0:T(8,128)(2,1)S(1)}, u32[]{:S(2)}, u32[]{:S(2)}) collective-permute-start(bf16[512,512]{1,0:T(8,128)(2,1)S(1)} %get-tuple-element.349), channel_id=1, source_target_pairs={{0,1},{1,2},{2,3},{3,4},{4,5},{5,6},{6,7},{7,8},{8,9},{9,10},{10,1... | collective-permute-start | bytes 1572872 | tf_op jit(solution)/shard_map/while/body/eval_jaxpr/ppermute | solution.py:30
  42.2 10.1 %collective-permute-start.1 = (bf16[512,32]{0,1:T(8,128)(2,1)S(1)}, bf16[512,32]{0,1:T(8,128)(2,1)S(1)}, u32[]{:S(2)}, u32[]{:S(2)}) collective-permute-start(bf16[512,32]{0,1:T(8,128)(2,1)S(1)} %get-tuple-element.350), channel_id=1, source_target_pairs={{0,1},{1,2},{2,3},{3,4},{4,5},{5,6},{6,7},{7,8},{8,9},{9,10},{10,1... | collective-permute-start | bytes 98312 | tf_op jit(solution)/shard_map/while/body/eval_jaxpr/ppermute | solution.py:31
  56.3 10.2 %collective-permute-start = (bf16[512,512]{1,0:T(8,128)(2,1)S(1)}, bf16[512,512]{1,0:T(8,128)(2,1)S(1)}, u32[]{:S(2)}, u32[]{:S(2)}) collective-permute-start(bf16[512,512]{1,0:T(8,128)(2,1)S(1)} %get-tuple-element.349), channel_id=1, source_target_pairs={{0,1},{1,2},{2,3},{3,4},{4,5},{5,6},{6,7},{7,8},{8,9},{9,10},{10,1... | collective-permute-start | bytes 1572872 | tf_op jit(solution)/shard_map/while/body/eval_jaxpr/ppermute | solution.py:30
  56.4 10.1 %collective-permute-start.1 = (bf16[512,32]{0,1:T(8,128)(2,1)S(1)}, bf16[512,32]{0,1:T(8,128)(2,1)S(1)}, u32[]{:S(2)}, u32[]{:S(2)}) collective-permute-start(bf16[512,32]{0,1:T(8,128)(2,1)S(1)} %get-tuple-element.350), channel_id=1, source_target_pairs={{0,1},{1,2},{2,3},{3,4},{4,5},{5,6},{6,7},{7,8},{8,9},{9,10},{10,1... | collective-permute-start | bytes 98312 | tf_op jit(solution)/shard_map/while/body/eval_jaxpr/ppermute | solution.py:31
  70.5 10.2 %collective-permute-start = (bf16[512,512]{1,0:T(8,128)(2,1)S(1)}, bf16[512,512]{1,0:T(8,128)(2,1)S(1)}, u32[]{:S(2)}, u32[]{:S(2)}) collective-permute-start(bf16[512,512]{1,0:T(8,128)(2,1)S(1)} %get-tuple-element.349), channel_id=1, source_target_pairs={{0,1},{1,2},{2,3},{3,4},{4,5},{5,6},{6,7},{7,8},{8,9},{9,10},{10,1... | collective-permute-start | bytes 1572872 | tf_op jit(solution)/shard_map/while/body/eval_jaxpr/ppermute | solution.py:30
  70.6 10.1 %collective-permute-start.1 = (bf16[512,32]{0,1:T(8,128)(2,1)S(1)}, bf16[512,32]{0,1:T(8,128)(2,1)S(1)}, u32[]{:S(2)}, u32[]{:S(2)}) collective-permute-start(bf16[512,32]{0,1:T(8,128)(2,1)S(1)} %get-tuple-element.350), channel_id=1, source_target_pairs={{0,1},{1,2},{2,3},{3,4},{4,5},{5,6},{6,7},{7,8},{8,9},{9,10},{10,1... | collective-permute-start | bytes 98312 | tf_op jit(solution)/shard_map/while/body/eval_jaxpr/ppermute | solution.py:31
  84.7 10.2 %collective-permute-start = (bf16[512,512]{1,0:T(8,128)(2,1)S(1)}, bf16[512,512]{1,0:T(8,128)(2,1)S(1)}, u32[]{:S(2)}, u32[]{:S(2)}) collective-permute-start(bf16[512,512]{1,0:T(8,128)(2,1)S(1)} %get-tuple-element.349), channel_id=1, source_target_pairs={{0,1},{1,2},{2,3},{3,4},{4,5},{5,6},{6,7},{7,8},{8,9},{9,10},{10,1... | collective-permute-start | bytes 1572872 | tf_op jit(solution)/shard_map/while/body/eval_jaxpr/ppermute | solution.py:30
  98.9 10.2 %collective-permute-start = (bf16[512,512]{1,0:T(8,128)(2,1)S(1)}, bf16[512,512]{1,0:T(8,128)(2,1)S(1)}, u32[]{:S(2)}, u32[]{:S(2)}) collective-permute-start(bf16[512,512]{1,0:T(8,128)(2,1)S(1)} %get-tuple-element.349), channel_id=1, source_target_pairs={{0,1},{1,2},{2,3},{3,4},{4,5},{5,6},{6,7},{7,8},{8,9},{9,10},{10,1... | collective-permute-start | bytes 1572872 | tf_op jit(solution)/shard_map/while/body/eval_jaxpr/ppermute | solution.py:30
  98.9 10.1 %collective-permute-start.1 = (bf16[512,32]{0,1:T(8,128)(2,1)S(1)}, bf16[512,32]{0,1:T(8,128)(2,1)S(1)}, u32[]{:S(2)}, u32[]{:S(2)}) collective-permute-start(bf16[512,32]{0,1:T(8,128)(2,1)S(1)} %get-tuple-element.350), channel_id=1, source_target_pairs={{0,1},{1,2},{2,3},{3,4},{4,5},{5,6},{6,7},{7,8},{8,9},{9,10},{10,1... | collective-permute-start | bytes 98312 | tf_op jit(solution)/shard_map/while/body/eval_jaxpr/ppermute | solution.py:31
  113.1 10.2 %collective-permute-start = (bf16[512,512]{1,0:T(8,128)(2,1)S(1)}, bf16[512,512]{1,0:T(8,128)(2,1)S(1)}, u32[]{:S(2)}, u32[]{:S(2)}) collective-permute-start(bf16[512,512]{1,0:T(8,128)(2,1)S(1)} %get-tuple-element.349), channel_id=1, source_target_pairs={{0,1},{1,2},{2,3},{3,4},{4,5},{5,6},{6,7},{7,8},{8,9},{9,10},{10,1... | collective-permute-start | bytes 1572872 | tf_op jit(solution)/shard_map/while/body/eval_jaxpr/ppermute | solution.py:30
  113.1 10.1 %collective-permute-start.1 = (bf16[512,32]{0,1:T(8,128)(2,1)S(1)}, bf16[512,32]{0,1:T(8,128)(2,1)S(1)}, u32[]{:S(2)}, u32[]{:S(2)}) collective-permute-start(bf16[512,32]{0,1:T(8,128)(2,1)S(1)} %get-tuple-element.350), channel_id=1, source_target_pairs={{0,1},{1,2},{2,3},{3,4},{4,5},{5,6},{6,7},{7,8},{8,9},{9,10},{10,1... | collective-permute-start | bytes 98312 | tf_op jit(solution)/shard_map/while/body/eval_jaxpr/ppermute | solution.py:31
  127.2 10.2 %collective-permute-start = (bf16[512,512]{1,0:T(8,128)(2,1)S(1)}, bf16[512,512]{1,0:T(8,128)(2,1)S(1)}, u32[]{:S(2)}, u32[]{:S(2)}) collective-permute-start(bf16[512,512]{1,0:T(8,128)(2,1)S(1)} %get-tuple-element.349), channel_id=1, source_target_pairs={{0,1},{1,2},{2,3},{3,4},{4,5},{5,6},{6,7},{7,8},{8,9},{9,10},{10,1... | collective-permute-start | bytes 1572872 | tf_op jit(solution)/shard_map/while/body/eval_jaxpr/ppermute | solution.py:30
  127.3 10.1 %collective-permute-start.1 = (bf16[512,32]{0,1:T(8,128)(2,1)S(1)}, bf16[512,32]{0,1:T(8,128)(2,1)S(1)}, u32[]{:S(2)}, u32[]{:S(2)}) collective-permute-start(bf16[512,32]{0,1:T(8,128)(2,1)S(1)} %get-tuple-element.350), channel_id=1, source_target_pairs={{0,1},{1,2},{2,3},{3,4},{4,5},{5,6},{6,7},{7,8},{8,9},{9,10},{10,1... | collective-permute-start | bytes 98312 | tf_op jit(solution)/shard_map/while/body/eval_jaxpr/ppermute | solution.py:31
  141.4 10.2 %collective-permute-start = (bf16[512,512]{1,0:T(8,128)(2,1)S(1)}, bf16[512,512]{1,0:T(8,128)(2,1)S(1)}, u32[]{:S(2)}, u32[]{:S(2)}) collective-permute-start(bf16[512,512]{1,0:T(8,128)(2,1)S(1)} %get-tuple-element.349), channel_id=1, source_target_pairs={{0,1},{1,2},{2,3},{3,4},{4,5},{5,6},{6,7},{7,8},{8,9},{9,10},{10,1... | collective-permute-start | bytes 1572872 | tf_op jit(solution)/shard_map/while/body/eval_jaxpr/ppermute | solution.py:30
  141.5 10.1 %collective-permute-start.1 = (bf16[512,32]{0,1:T(8,128)(2,1)S(1)}, bf16[512,32]{0,1:T(8,128)(2,1)S(1)}, u32[]{:S(2)}, u32[]{:S(2)}) collective-permute-start(bf16[512,32]{0,1:T(8,128)(2,1)S(1)} %get-tuple-element.350), channel_id=1, source_target_pairs={{0,1},{1,2},{2,3},{3,4},{4,5},{5,6},{6,7},{7,8},{8,9},{9,10},{10,1... | collective-permute-start | bytes 98312 | tf_op jit(solution)/shard_map/while/body/eval_jaxpr/ppermute | solution.py:31
  155.6 10.2 %collective-permute-start = (bf16[512,512]{1,0:T(8,128)(2,1)S(1)}, bf16[512,512]{1,0:T(8,128)(2,1)S(1)}, u32[]{:S(2)}, u32[]{:S(2)}) collective-permute-start(bf16[512,512]{1,0:T(8,128)(2,1)S(1)} %get-tuple-element.349), channel_id=1, source_target_pairs={{0,1},{1,2},{2,3},{3,4},{4,5},{5,6},{6,7},{7,8},{8,9},{9,10},{10,1... | collective-permute-start | bytes 1572872 | tf_op jit(solution)/shard_map/while/body/eval_jaxpr/ppermute | solution.py:30
  169.8 10.2 %collective-permute-start = (bf16[512,512]{1,0:T(8,128)(2,1)S(1)}, bf16[512,512]{1,0:T(8,128)(2,1)S(1)}, u32[]{:S(2)}, u32[]{:S(2)}) collective-permute-start(bf16[512,512]{1,0:T(8,128)(2,1)S(1)} %get-tuple-element.349), channel_id=1, source_target_pairs={{0,1},{1,2},{2,3},{3,4},{4,5},{5,6},{6,7},{7,8},{8,9},{9,10},{10,1... | collective-permute-start | bytes 1572872 | tf_op jit(solution)/shard_map/while/body/eval_jaxpr/ppermute | solution.py:30
  184.0 10.2 %collective-permute-start = (bf16[512,512]{1,0:T(8,128)(2,1)S(1)}, bf16[512,512]{1,0:T(8,128)(2,1)S(1)}, u32[]{:S(2)}, u32[]{:S(2)}) collective-permute-start(bf16[512,512]{1,0:T(8,128)(2,1)S(1)} %get-tuple-element.349), channel_id=1, source_target_pairs={{0,1},{1,2},{2,3},{3,4},{4,5},{5,6},{6,7},{7,8},{8,9},{9,10},{10,1... | collective-permute-start | bytes 1572872 | tf_op jit(solution)/shard_map/while/body/eval_jaxpr/ppermute | solution.py:30
  198.2 10.2 %collective-permute-start = (bf16[512,512]{1,0:T(8,128)(2,1)S(1)}, bf16[512,512]{1,0:T(8,128)(2,1)S(1)}, u32[]{:S(2)}, u32[]{:S(2)}) collective-permute-start(bf16[512,512]{1,0:T(8,128)(2,1)S(1)} %get-tuple-element.349), channel_id=1, source_target_pairs={{0,1},{1,2},{2,3},{3,4},{4,5},{5,6},{6,7},{7,8},{8,9},{9,10},{10,1... | collective-permute-start | bytes 1572872 | tf_op jit(solution)/shard_map/while/body/eval_jaxpr/ppermute | solution.py:30
  212.4 10.2 %collective-permute-start = (bf16[512,512]{1,0:T(8,128)(2,1)S(1)}, bf16[512,512]{1,0:T(8,128)(2,1)S(1)}, u32[]{:S(2)}, u32[]{:S(2)}) collective-permute-start(bf16[512,512]{1,0:T(8,128)(2,1)S(1)} %get-tuple-element.349), channel_id=1, source_target_pairs={{0,1},{1,2},{2,3},{3,4},{4,5},{5,6},{6,7},{7,8},{8,9},{9,10},{10,1... | collective-permute-start | bytes 1572872 | tf_op jit(solution)/shard_map/while/body/eval_jaxpr/ppermute | solution.py:30
  (8 other events, 68.4 us)
where the time goes:
time: 228 us; the launch traced here: 227 us
  waiting for transfers between devices  143 us (63%)
  matrix products  59 us (26%)
  local copies, waits for them, and re-layouts  13.1 us (6%)
  other arithmetic  5.54 us (2%)
  starting transfers between devices  4.11 us (2%)
    ppermute x15, waiting for transfers between devices, shift_step(): v_cur = lax.ppermute(v_cur, 'sp', shift_pairs)  143 us
    dot_general x16, matrix products, block_product(): return jnp.dot(kern_blk, v_rows, preferred_element_type=jnp.float32)  59 us
    dynamic_slice x15, local copies, waits for them, and re-layouts, shift_step(): return (x_cur, v_cur, y_acc + part_y * weights[src_block])  9.19 us
  transfers between devices with their start and end apart: 30, of which 15 were waited for; matrix products, arithmetic and copies ran while one was open for 4% of the time, Pallas kernels for 0%

commit v1 on v0

v1 whole, which is shorter than its diff:
```python
import functools
import math

import jax
import jax.numpy as jnp
from jax import lax
from jax.experimental import pallas as pl
from jax.experimental.pallas import tpu as pltpu
from jax.sharding import PartitionSpec as P

F32 = jnp.float32
BF16 = jnp.bfloat16
MESH = pl.DeviceIdType.MESH
LOG2_E = math.log2(math.e)
TILE = 256
LANES = 128


def kernel(n_dev, z_hbm, x_hbm, v_hbm, mask_hbm, ell_hbm, scl_hbm, y_ref,
           z_in, zt, xs, v_in, nzh, crow, mask_s, ell_s, scl_s,
           load_sem, ring_send, ring_recv, sib_send, sib_recv, own_send, own_recv):
    n_chip = n_dev // 2
    n_step = n_chip - 1
    mz, d = z_hbm.shape
    nx, r = v_hbm.shape
    half_rows = nx // 2
    vrows = r * half_rows // d
    q_rows = half_rows // 2
    pieces = ((0, vrows + q_rows), (vrows + q_rows, q_rows))

    me = lax.axis_index("sp")
    chip, core = me // 2, me % 2
    right = ((chip + 1) % n_chip) * 2 + core
    left = ((chip + n_chip - 1) % n_chip) * 2 + core
    sib = chip * 2 + (1 - core)

    barrier = pltpu.get_barrier_semaphore()
    for peer in (right, left, sib):
        pl.semaphore_signal(barrier, inc=1, device_id={"sp": peer}, device_id_type=MESH)

    loads = [
        pltpu.make_async_copy(v_hbm, v_in, load_sem.at[0]),
        pltpu.make_async_copy(x_hbm.at[pl.ds(0, half_rows)], xs.at[me, 0, pl.ds(vrows, half_rows)], load_sem.at[1]),
        pltpu.make_async_copy(x_hbm.at[pl.ds(half_rows, half_rows)], xs.at[me, 1, pl.ds(vrows, half_rows)], load_sem.at[2]),
        pltpu.make_async_copy(z_hbm, z_in, load_sem.at[3]),
        pltpu.make_async_copy(mask_hbm, mask_s, load_sem.at[4]),
        pltpu.make_async_copy(ell_hbm, ell_s, load_sem.at[5]),
        pltpu.make_async_copy(scl_hbm, scl_s, load_sem.at[6]),
    ]
    for load in loads:
        load.start()

    loads[0].wait()
    vt = v_in[...].astype(F32).T.astype(BF16)
    for half in range(2):
        cols = vt[:, half * half_rows:(half + 1) * half_rows]
        xs[me, half, 0:vrows, :] = jnp.concatenate([cols[b * vrows:(b + 1) * vrows] for b in range(r // vrows)], axis=1)

    def remote(src_dst, send_sem, recv_sem, peer):
        return pltpu.make_async_remote_copy(
            src_ref=src_dst, dst_ref=src_dst, send_sem=send_sem, recv_sem=recv_sem,
            device_id={"sp": peer}, device_id_type=MESH)

    def piece(j, half, q):
        return xs.at[j, half, pl.ds(*pieces[q])]

    def to_right(s, q):
        j = ((chip + n_chip - s // 2) % n_chip) * 2 + core
        return remote(piece(j, s % 2, q), ring_send.at[0, s, q], ring_recv.at[0, s, q], right)

    def to_left(s, q):
        j = ((chip + s // 2) % n_chip) * 2 + core
        return remote(piece(j, 1 - s % 2, q), ring_send.at[1, s, q], ring_recv.at[1, s, q], left)

    def source(u, c):
        h = u // 2 + 1
        return (((chip + n_chip - h) % n_chip) * 2 + c, u % 2), (((chip + h) % n_chip) * 2 + c, 1 - u % 2)

    def from_ring(u, q):
        a, b = source(u, core)
        return (remote(piece(*a, q), ring_send.at[0, u, q], ring_recv.at[0, u, q], left),
                remote(piece(*b, q), ring_send.at[1, u, q], ring_recv.at[1, u, q], right))

    def sibling(u, q, c):
        a, b = source(u, c)
        return (remote(piece(*a, q), sib_send.at[0, u, q], sib_recv.at[0, u, q], sib),
                remote(piece(*b, q), sib_send.at[1, u, q], sib_recv.at[1, u, q], sib))

    def own(j, half):
        return remote(xs.at[j, half], own_send.at[half], own_recv.at[half], sib)

    loads[1].wait()
    loads[2].wait()
    pl.semaphore_wait(barrier, 3)
    for s in range(2):
        for q in range(2):
            to_right(s, q).start()
            to_left(s, q).start()
    for half in range(2):
        own(me, half).start()

    loads[5].wait()
    loads[6].wait()
    loads[4].wait()
    ell = jnp.full((8, TILE), ell_s[0], F32)
    crow[...] = (-LOG2_E) / (ell * ell)
    loads[3].wait()
    for t in range(mz // TILE):
        zt_t = z_in[t * TILE:(t + 1) * TILE, :].T
        zt[:, t * TILE:(t + 1) * TILE] = zt_t
        zf = zt_t.astype(F32)
        nzh[:, t * TILE:(t + 1) * TILE] = jnp.broadcast_to(
            0.5 * jnp.sum(zf * zf, axis=0, keepdims=True), (8, TILE))
    y_ref[...] = jnp.zeros_like(y_ref)

    def weighted(j, half, lane0, width):
        v_rows = jnp.concatenate(
            [xs[j, half, 0:vrows, b * half_rows + lane0:b * half_rows + lane0 + width] for b in range(r // vrows)], axis=0)
        return (v_rows.astype(F32) * mask_s[0, j].astype(F32)).astype(BF16)

    def accumulate(x, vt_x):
        xf = x.astype(F32)
        nxh = 0.5 * jnp.sum(xf * xf, axis=1, keepdims=True)
        scale = scl_s[0]
        for t in range(mz // TILE):
            cols = slice(t * TILE, (t + 1) * TILE)
            gram = jnp.dot(x, zt[:, cols], preferred_element_type=F32)
            half_dist = jnp.maximum(nzh[0:1, cols] + nxh - gram, 0.0)
            kern = (scale * jnp.exp2(half_dist * crow[0:1, :])).astype(BF16)
            y_ref[:, cols] += jnp.dot(vt_x, kern, preferred_element_type=F32)

    def use_half(j, half):
        accumulate(xs[j, half, vrows:vrows + half_rows, :], weighted(j, half, 0, half_rows))

    def use_pair(u, q, c):
        a, b = source(u, c)
        x = jnp.concatenate([xs[a[0], a[1], pl.ds(vrows + q * q_rows, q_rows), :],
                             xs[b[0], b[1], pl.ds(vrows + q * q_rows, q_rows), :]], axis=0)
        vt_x = jnp.concatenate([weighted(*a, q * q_rows, q_rows), weighted(*b, q * q_rows, q_rows)], axis=1)
        accumulate(x, vt_x)

    @pl.loop(0, 2)
    def _(half):
        use_half(me, half)

    @pl.loop(0, 2)
    def _(half):
        own(sib, half).wait_recv()
        use_half(sib, half)

    @pl.loop(0, n_step)
    def _(u):
        for q in range(2):
            ring = from_ring(u, q)
            to_sib = sibling(u, q, core)
            for k in range(2):
                ring[k].wait_recv()

                @pl.when(u < n_step - 2)
                def _():
                    (to_right, to_left)[k](u + 2, q).start()

                to_sib[k].start()
            use_pair(u, q, core)
            for copy in sibling(u, q, 1 - core):
                copy.wait_recv()
            use_pair(u, q, 1 - core)

    for half in range(2):
        own(me, half).wait_send()

    @pl.loop(0, n_step)
    def _(u):
        for q in range(2):
            to_right(u, q).wait_send()
            to_left(u, q).wait_send()
            for copy in sibling(u, q, core):
                copy.wait_send()


def solution(mesh):
    n_dev = mesh.shape["sp"]
    n_step = n_dev // 2 - 1
    row_spec = P(("dp", "sp"), None)

    def local_fn(z_rows, x_rows, v_rows, mask_row, length_scale, out_scale):
        mz, d = z_rows.shape
        nx, r = v_rows.shape
        slot_rows = nx // 2 + r * nx // 2 // d
        dma = pltpu.SemaphoreType.DMA
        y_t = pl.pallas_call(
            functools.partial(kernel, n_dev),
            name="ring_predict",
            out_shape=jax.ShapeDtypeStruct((r, mz), F32),
            in_specs=[pl.BlockSpec(memory_space=pl.ANY)] * 6,
            out_specs=pl.BlockSpec(memory_space=pltpu.VMEM),
            scratch_shapes=[
                pltpu.VMEM((mz, d), BF16),
                pltpu.VMEM((d, mz), BF16),
                pltpu.VMEM((n_dev, 2, slot_rows, d), BF16),
                pltpu.VMEM((nx, r), BF16),
                pltpu.VMEM((8, mz), F32),
                pltpu.VMEM((8, TILE), F32),
                pltpu.SMEM((1, n_dev), jnp.int32),
                pltpu.SMEM((1,), F32),
                pltpu.SMEM((1,), F32),
                dma((7,)),
                dma((2, n_step, 2)), dma((2, n_step, 2)),
                dma((2, n_step, 2)), dma((2, n_step, 2)),
                dma((2,)), dma((2,)),
            ],
            compiler_params=pltpu.CompilerParams(
                collective_id=0, has_side_effects=True, vmem_limit_bytes=60 * 1024 * 1024),
        )(z_rows, x_rows, v_rows, mask_row, length_scale, out_scale)
        return y_t.T

    return jax.shard_map(local_fn, mesh=mesh, in_specs=(row_spec, row_spec, row_spec, row_spec, P(None), P(None)), out_specs=row_spec, check_vma=False)
```

time: 228 us -> 93.6 us (0.41)
  the two profiles are of different devices: /device:TPU:22 before, /device:TPU:21 now
where the time goes in v1:
time: 93.6 us; the launch traced here: 93.3 us
  Pallas kernels  88.9 us (95%)
  local copies, waits for them, and re-layouts  3.19 us (3%)
  between operations  1.31 us (1%)
    pallas_call x1, Pallas kernels, local_fn(): pl.pallas_call(functools.partial(kernel, n_dev), name='ring_predict', out...  88.9 us
    unnamed x2, local copies, waits for them, and re-layouts  3.19 us

profile of v1, /device:TPU:21, one launch (start us, length us, event | category | flops | bytes accessed | tf_op | source)
XLA Modules:
  0.0 93.3 jit_solution(7832688856596828186)
XLA Ops:
  1.3 1.5 %copy.7.v_hbm = bf16[512,32]{1,0:T(8,128)(2,1)} copy(bf16[512,32]{0,1:T(8,128)(2,1)} %param.8) | data formatting | bytes 65536 | tf_op args[2]
  2.8 88.9 %ring_predict.1 = f32[32,2048]{1,0:T(8,128)} custom-call(bf16[2048,512]{1,0:T(8,128)(2,1)} %z_hbm.1, bf16[512,512]{1,0:T(8,128)(2,1)} %x_hbm.1, bf16[512,32]{1,0:T(8,128)(2,1)} %copy.7.v_hbm, s32[1,16]{1,0:T(1,128)} %mask_hbm.1, f32[1]{0:T(128)S(6)} %copy.9.ell_hbm, f32[1]{0:T(128)S(6)} %copy.10.scl_hbm), custom_call_target="tpu_custom_call" | custom-call | tf_op jit(solution)/shard_map/ring_predict/pallas_call | solution.py:191
  91.7 1.7 %copy.11 = f32[2048,32]{0,1:T(8,128)} copy(f32[2048,32]{0,1:T(8,128)} %bitcast.1) | data formatting | bytes 524288

commit v2 on v1

--- a/solution.py
+++ b/solution.py
@@ -12,17 +12,17 @@
 BF16 = jnp.bfloat16
 MESH = pl.DeviceIdType.MESH
 LOG2_E = math.log2(math.e)
-TILE = 256
+TILE = 512
 LANES = 128
 
 
 def kernel(n_dev, z_hbm, x_hbm, v_hbm, mask_hbm, ell_hbm, scl_hbm, y_ref,
-           z_in, zt, xs, v_in, nzh, crow, mask_s, ell_s, scl_s,
-           load_sem, ring_send, ring_recv, sib_send, sib_recv, own_send, own_recv):
+           z_in, zt, xs, nzh, crow, mask_s, ell_s, scl_s,
+           nx_s, load_sem, ring_send, ring_recv, sib_send, sib_recv, own_send, own_recv):
     n_chip = n_dev // 2
     n_step = n_chip - 1
     mz, d = z_hbm.shape
-    nx, r = v_hbm.shape
+    r, nx = v_hbm.shape
     half_rows = nx // 2
     vrows = r * half_rows // d
     q_rows = half_rows // 2
@@ -38,23 +38,20 @@
     for peer in (right, left, sib):
         pl.semaphore_signal(barrier, inc=1, device_id={"sp": peer}, device_id_type=MESH)
 
-    loads = [
-        pltpu.make_async_copy(v_hbm, v_in, load_sem.at[0]),
-        pltpu.make_async_copy(x_hbm.at[pl.ds(0, half_rows)], xs.at[me, 0, pl.ds(vrows, half_rows)], load_sem.at[1]),
-        pltpu.make_async_copy(x_hbm.at[pl.ds(half_rows, half_rows)], xs.at[me, 1, pl.ds(vrows, half_rows)], load_sem.at[2]),
-        pltpu.make_async_copy(z_hbm, z_in, load_sem.at[3]),
-        pltpu.make_async_copy(mask_hbm, mask_s, load_sem.at[4]),
-        pltpu.make_async_copy(ell_hbm, ell_s, load_sem.at[5]),
-        pltpu.make_async_copy(scl_hbm, scl_s, load_sem.at[6]),
+    loads = [pltpu.make_async_copy(x_hbm.at[pl.ds(half * half_rows, half_rows)],
+                                   xs.at[me, half, pl.ds(vrows, half_rows)], load_sem.at[half]) for half in range(2)]
+    loads += [pltpu.make_async_copy(v_hbm.at[pl.ds(b * vrows, vrows), pl.ds(half * half_rows, half_rows)],
+                                    xs.at[me, half, pl.ds(0, vrows), pl.ds(b * half_rows, half_rows)],
+                                    load_sem.at[2 + 2 * half + b]) for half in range(2) for b in range(2)]
+    n_own = len(loads)
+    loads += [
+        pltpu.make_async_copy(mask_hbm, mask_s, load_sem.at[n_own]),
+        pltpu.make_async_copy(ell_hbm, ell_s, load_sem.at[n_own + 1]),
+        pltpu.make_async_copy(scl_hbm, scl_s, load_sem.at[n_own + 2]),
+        pltpu.make_async_copy(z_hbm, z_in, load_sem.at[n_own + 3]),
     ]
     for load in loads:
         load.start()
-
-    loads[0].wait()
-    vt = v_in[...].astype(F32).T.astype(BF16)
-    for half in range(2):
-        cols = vt[:, half * half_rows:(half + 1) * half_rows]
-        xs[me, half, 0:vrows, :] = jnp.concatenate([cols[b * vrows:(b + 1) * vrows] for b in range(r // vrows)], axis=1)
 
     def remote(src_dst, send_sem, recv_sem, peer):
         return pltpu.make_async_remote_copy(
@@ -89,8 +86,8 @@
     def own(j, half):
         return remote(xs.at[j, half], own_send.at[half], own_recv.at[half], sib)
 
-    loads[1].wait()
-    loads[2].wait()
+    for load in loads[:n_own]:
+        load.wait()
     pl.semaphore_wait(barrier, 3)
     for s in range(2):
         for q in range(2):
@@ -99,12 +96,10 @@
     for half in range(2):
         own(me, half).start()
 
-    loads[5].wait()
-    loads[6].wait()
-    loads[4].wait()
+    for load in loads[n_own:]:
+        load.wait()
     ell = jnp.full((8, TILE), ell_s[0], F32)
     crow[...] = (-LOG2_E) / (ell * ell)
-    loads[3].wait()
     for t in range(mz // TILE):
         zt_t = z_in[t * TILE:(t + 1) * TILE, :].T
         zt[:, t * TILE:(t + 1) * TILE] = zt_t
@@ -120,12 +115,15 @@
 
     def accumulate(x, vt_x):
         xf = x.astype(F32)
-        nxh = 0.5 * jnp.sum(xf * xf, axis=1, keepdims=True)
+        nx_s[...] = jnp.broadcast_to(0.5 * jnp.sum(xf * xf, axis=1, keepdims=True), nx_s.shape)
         scale = scl_s[0]
-        for t in range(mz // TILE):
-            cols = slice(t * TILE, (t + 1) * TILE)
-            gram = jnp.dot(x, zt[:, cols], preferred_element_type=F32)
-            half_dist = jnp.maximum(nzh[0:1, cols] + nxh - gram, 0.0)
+        tiles = [slice(t * TILE, (t + 1) * TILE) for t in range(mz // TILE)]
+        ahead = jnp.dot(x, zt[:, tiles[0]], preferred_element_type=F32)
+        for t, cols in enumerate(tiles):
+            gram = ahead
+            if t + 1 < len(tiles):
+                ahead = jnp.dot(x, zt[:, tiles[t + 1]], preferred_element_type=F32)
+            half_dist = jnp.maximum(nzh[0:1, cols] + jnp.concatenate([nx_s[...]] * (TILE // LANES), axis=1) - gram, 0.0)
             kern = (scale * jnp.exp2(half_dist * crow[0:1, :])).astype(BF16)
             y_ref[:, cols] += jnp.dot(vt_x, kern, preferred_element_type=F32)
 
@@ -198,20 +196,20 @@
                 pltpu.VMEM((mz, d), BF16),
                 pltpu.VMEM((d, mz), BF16),
                 pltpu.VMEM((n_dev, 2, slot_rows, d), BF16),
-                pltpu.VMEM((nx, r), BF16),
                 pltpu.VMEM((8, mz), F32),
                 pltpu.VMEM((8, TILE), F32),
                 pltpu.SMEM((1, n_dev), jnp.int32),
                 pltpu.SMEM((1,), F32),
                 pltpu.SMEM((1,), F32),
-                dma((7,)),
+                pltpu.VMEM((nx // 2, LANES), F32),
+                dma((10,)),
                 dma((2, n_step, 2)), dma((2, n_step, 2)),
                 dma((2, n_step, 2)), dma((2, n_step, 2)),
                 dma((2,)), dma((2,)),
             ],
             compiler_params=pltpu.CompilerParams(
                 collective_id=0, has_side_effects=True, vmem_limit_bytes=60 * 1024 * 1024),
-        )(z_rows, x_rows, v_rows, mask_row, length_scale, out_scale)
+        )(z_rows, x_rows, v_rows.T, mask_row, length_scale, out_scale)
         return y_t.T
 
     return jax.shard_map(local_fn, mesh=mesh, in_specs=(row_spec, row_spec, row_spec, row_spec, P(None), P(None)), out_specs=row_spec, check_vma=False)

time: 93.6 us -> 59.6 us (0.64)
  Pallas kernels: 88.9 us -> 56.5 us
  local copies, waits for them, and re-layouts: 3.19 us -> 1.67 us
    pallas_call x1, Pallas kernels: 88.9 us -> 56.5 us  [local_fn(): pl.pallas_call(functools.partial(kernel, n_dev), name='ring_predict', out...]
    unnamed x2 -> x1, local copies, waits for them, and re-layouts: 3.19 us -> 1.67 us
where the time goes in v2:
time: 59.6 us; the launch traced here: 59.4 us
  Pallas kernels  56.5 us (95%)
  local copies, waits for them, and re-layouts  1.67 us (3%)
  between operations  1.3 us (2%)
    pallas_call x1, Pallas kernels, local_fn(): pl.pallas_call(functools.partial(kernel, n_dev), name='ring_predict', out...  56.5 us
    unnamed x1, local copies, waits for them, and re-layouts  1.67 us

profile of v2, /device:TPU:21, one launch (start us, length us, event | category | flops | bytes accessed | tf_op | source)
XLA Modules:
  0.0 59.4 jit_solution(15956804903384973065)
XLA Ops:
  1.3 56.5 %ring_predict.1 = f32[32,2048]{1,0:T(8,128)} custom-call(bf16[2048,512]{1,0:T(8,128)(2,1)} %z_hbm.1, bf16[512,512]{1,0:T(8,128)(2,1)} %x_hbm.1, bf16[32,512]{1,0:T(8,128)(2,1)} %bitcast.3, s32[1,16]{1,0:T(1,128)} %mask_hbm.1, f32[1]{0:T(128)S(6)} %copy.8.ell_hbm, f32[1]{0:T(128)S(6)} %copy.9.scl_hbm), custom_call_target="tpu_custom_call" | custom-call | tf_op jit(solution)/shard_map/ring_predict/pallas_call | solution.py:189
  57.8 1.7 %copy.10 = f32[2048,32]{0,1:T(8,128)} copy(f32[2048,32]{0,1:T(8,128)} %bitcast.2) | data formatting | bytes 524288

commit v3 on v2

--- a/solution.py
+++ b/solution.py
@@ -16,17 +16,17 @@
 LANES = 128
 
 
-def kernel(n_dev, z_hbm, x_hbm, v_hbm, mask_hbm, ell_hbm, scl_hbm, y_ref,
-           z_in, zt, xs, nzh, crow, mask_s, ell_s, scl_s,
-           nx_s, load_sem, ring_send, ring_recv, sib_send, sib_recv, own_send, own_recv):
+def kernel(n_dev, z_hbm, x_hbm, v_hbm, mask_hbm, ell_s, scl_s, y_ref,
+           z_in, zt, xs, nzh, crow, mask_s, nx_s,
+           load_sem, ring_send, ring_recv, sib_send, sib_recv, own_send, own_recv):
     n_chip = n_dev // 2
     n_step = n_chip - 1
     mz, d = z_hbm.shape
     r, nx = v_hbm.shape
     half_rows = nx // 2
     vrows = r * half_rows // d
-    q_rows = half_rows // 2
-    pieces = ((0, vrows + q_rows), (vrows + q_rows, q_rows))
+    spans = ((0, half_rows // 2), (half_rows // 2, half_rows // 4), (3 * half_rows // 4, half_rows // 4))
+    n_piece = len(spans)
 
     me = lax.axis_index("sp")
     chip, core = me // 2, me % 2
@@ -46,9 +46,7 @@
     n_own = len(loads)
     loads += [
         pltpu.make_async_copy(mask_hbm, mask_s, load_sem.at[n_own]),
-        pltpu.make_async_copy(ell_hbm, ell_s, load_sem.at[n_own + 1]),
-        pltpu.make_async_copy(scl_hbm, scl_s, load_sem.at[n_own + 2]),
-        pltpu.make_async_copy(z_hbm, z_in, load_sem.at[n_own + 3]),
+        pltpu.make_async_copy(z_hbm, z_in, load_sem.at[n_own + 1]),
     ]
     for load in loads:
         load.start()
@@ -59,7 +57,8 @@
             device_id={"sp": peer}, device_id_type=MESH)
 
     def piece(j, half, q):
-        return xs.at[j, half, pl.ds(*pieces[q])]
+        lo, rows = spans[q]
+        return xs.at[j, half, pl.ds(vrows + lo, rows) if q else pl.ds(0, vrows + rows)]
 
     def to_right(s, q):
         j = ((chip + n_chip - s // 2) % n_chip) * 2 + core
@@ -86,11 +85,21 @@
     def own(j, half):
         return remote(xs.at[j, half], own_send.at[half], own_recv.at[half], sib)
 
+    def ring_sent(s):
+        for q in range(n_piece):
+            for k in range(2):
+                remote(piece(0, 0, q), ring_send.at[k, s, q], ring_recv.at[k, s, q], right).wait_send()
+
+    def sibling_sent(u, qs):
+        for q in qs:
+            for k in range(2):
+                remote(piece(0, 0, q), sib_send.at[k, u, q], sib_recv.at[k, u, q], sib).wait_send()
+
     for load in loads[:n_own]:
         load.wait()
     pl.semaphore_wait(barrier, 3)
     for s in range(2):
-        for q in range(2):
+        for q in range(n_piece):
             to_right(s, q).start()
             to_left(s, q).start()
     for half in range(2):
@@ -108,14 +117,15 @@
             0.5 * jnp.sum(zf * zf, axis=0, keepdims=True), (8, TILE))
     y_ref[...] = jnp.zeros_like(y_ref)
 
-    def weighted(j, half, lane0, width):
+    def weighted(j, half, lo, rows):
         v_rows = jnp.concatenate(
-            [xs[j, half, 0:vrows, b * half_rows + lane0:b * half_rows + lane0 + width] for b in range(r // vrows)], axis=0)
+            [xs[j, half, 0:vrows, b * half_rows:(b + 1) * half_rows][:, lo:lo + rows] for b in range(r // vrows)], axis=0)
         return (v_rows.astype(F32) * mask_s[0, j].astype(F32)).astype(BF16)
 
     def accumulate(x, vt_x):
+        rows = x.shape[0]
         xf = x.astype(F32)
-        nx_s[...] = jnp.broadcast_to(0.5 * jnp.sum(xf * xf, axis=1, keepdims=True), nx_s.shape)
+        nx_s[0:rows, :] = jnp.broadcast_to(0.5 * jnp.sum(xf * xf, axis=1, keepdims=True), (rows, LANES))
         scale = scl_s[0]
         tiles = [slice(t * TILE, (t + 1) * TILE) for t in range(mz // TILE)]
         ahead = jnp.dot(x, zt[:, tiles[0]], preferred_element_type=F32)
@@ -123,19 +133,18 @@
             gram = ahead
             if t + 1 < len(tiles):
                 ahead = jnp.dot(x, zt[:, tiles[t + 1]], preferred_element_type=F32)
-            half_dist = jnp.maximum(nzh[0:1, cols] + jnp.concatenate([nx_s[...]] * (TILE // LANES), axis=1) - gram, 0.0)
+            nxh = jnp.concatenate([nx_s[0:rows, :]] * (TILE // LANES), axis=1)
+            half_dist = jnp.maximum(nzh[0:1, cols] + nxh - gram, 0.0)
             kern = (scale * jnp.exp2(half_dist * crow[0:1, :])).astype(BF16)
             y_ref[:, cols] += jnp.dot(vt_x, kern, preferred_element_type=F32)
 
     def use_half(j, half):
         accumulate(xs[j, half, vrows:vrows + half_rows, :], weighted(j, half, 0, half_rows))
 
-    def use_pair(u, q, c):
+    def use_pair(u, c, lo, rows):
         a, b = source(u, c)
-        x = jnp.concatenate([xs[a[0], a[1], pl.ds(vrows + q * q_rows, q_rows), :],
-                             xs[b[0], b[1], pl.ds(vrows + q * q_rows, q_rows), :]], axis=0)
-        vt_x = jnp.concatenate([weighted(*a, q * q_rows, q_rows), weighted(*b, q * q_rows, q_rows)], axis=1)
-        accumulate(x, vt_x)
+        x = jnp.concatenate([xs[a[0], a[1], pl.ds(vrows + lo, rows), :], xs[b[0], b[1], pl.ds(vrows + lo, rows), :]], axis=0)
+        accumulate(x, jnp.concatenate([weighted(*a, lo, rows), weighted(*b, lo, rows)], axis=1))
 
     @pl.loop(0, 2)
     def _(half):
@@ -146,34 +155,45 @@
         own(sib, half).wait_recv()
         use_half(sib, half)
 
-    @pl.loop(0, n_step)
-    def _(u):
-        for q in range(2):
-            ring = from_ring(u, q)
-            to_sib = sibling(u, q, core)
-            for k in range(2):
-                ring[k].wait_recv()
-
+    def arrive(u, q, forward):
+        ring = from_ring(u, q)
+        to_sib = sibling(u, q, core)
+        for k in range(2):
+            ring[k].wait_recv()
+            if forward:
                 @pl.when(u < n_step - 2)
                 def _():
                     (to_right, to_left)[k](u + 2, q).start()
 
-                to_sib[k].start()
-            use_pair(u, q, core)
-            for copy in sibling(u, q, 1 - core):
-                copy.wait_recv()
-            use_pair(u, q, 1 - core)
-
+            to_sib[k].start()
+
+    def step(u, groups, forward):
+        for qs in groups:
+            for q in qs:
+                arrive(u, q, forward)
+            lo, rows = spans[qs[0]][0], sum(spans[q][1] for q in qs)
+            use_pair(u, core, lo, rows)
+            for q in qs:
+                for copy in sibling(u, q, 1 - core):
+                    copy.wait_recv()
+            use_pair(u, 1 - core, lo, rows)
+
+    @pl.loop(0, n_step - 1)
+    def _(u):
+        step(u, ((0,), (1, 2)), True)
+
+        @pl.when(u > 0)
+        def _():
+            ring_sent(u - 1)
+            sibling_sent(u - 1, range(n_piece))
+
+    ring_sent(n_step - 2)
+    sibling_sent(n_step - 2, range(n_piece))
     for half in range(2):
         own(me, half).wait_send()
-
-    @pl.loop(0, n_step)
-    def _(u):
-        for q in range(2):
-            to_right(u, q).wait_send()
-            to_left(u, q).wait_send()
-            for copy in sibling(u, q, core):
-                copy.wait_send()
+    step(n_step - 1, ((0,), (1,), (2,)), False)
+    ring_sent(n_step - 1)
+    sibling_sent(n_step - 1, range(n_piece))
 
 
 def solution(mesh):
@@ -189,8 +209,8 @@
         y_t = pl.pallas_call(
             functools.partial(kernel, n_dev),
             name="ring_predict",
-            out_shape=jax.ShapeDtypeStruct((r, mz), F32),
-            in_specs=[pl.BlockSpec(memory_space=pl.ANY)] * 6,
+            out_shape=pltpu.VMEM((r, mz), F32),
+            in_specs=[pl.BlockSpec(memory_space=pl.ANY)] * 4 + [pl.BlockSpec(memory_space=pltpu.SMEM)] * 2,
             out_specs=pl.BlockSpec(memory_space=pltpu.VMEM),
             scratch_shapes=[
                 pltpu.VMEM((mz, d), BF16),
@@ -199,12 +219,10 @@
                 pltpu.VMEM((8, mz), F32),
                 pltpu.VMEM((8, TILE), F32),
                 pltpu.SMEM((1, n_dev), jnp.int32),
-                pltpu.SMEM((1,), F32),
-                pltpu.SMEM((1,), F32),
                 pltpu.VMEM((nx // 2, LANES), F32),
-                dma((10,)),
-                dma((2, n_step, 2)), dma((2, n_step, 2)),
-                dma((2, n_step, 2)), dma((2, n_step, 2)),
+                dma((8,)),
+                dma((2, n_step, 3)), dma((2, n_step, 3)),
+                dma((2, n_step, 3)), dma((2, n_step, 3)),
                 dma((2,)), dma((2,)),
             ],
             compiler_params=pltpu.CompilerParams(

time: 59.6 us -> 59.9 us (level)
  Pallas kernels: 56.5 us -> 57.8 us
  local copies, waits for them, and re-layouts: 1.67 us -> 0.71 us
    pallas_call x1, Pallas kernels: 56.5 us -> 57.8 us  [local_fn(): pl.pallas_call(functools.partial(kernel, n_dev), name='ring_predict', out...]
    unnamed x1, local copies, waits for them, and re-layouts: 1.67 us -> 0.71 us
where the time goes in v3:
time: 59.9 us; the launch traced here: 59.8 us
  Pallas kernels  57.8 us (96%)
  between operations  1.3 us (2%)
  local copies, waits for them, and re-layouts  0.71 us (1%)
    pallas_call x1, Pallas kernels, local_fn(): pl.pallas_call(functools.partial(kernel, n_dev), name='ring_predict', out...  57.8 us

profile of v3, /device:TPU:21, one launch (start us, length us, event | category | flops | bytes accessed | tf_op | source)
XLA Modules:
  0.0 59.8 jit_solution(6067045430089491016)
XLA Ops:
  1.3 57.8 %ring_predict.1 = f32[32,2048]{1,0:T(8,128)S(1)} custom-call(bf16[2048,512]{1,0:T(8,128)(2,1)} %z_hbm.1, bf16[512,512]{1,0:T(8,128)(2,1)} %x_hbm.1, bf16[32,512]{1,0:T(8,128)(2,1)} %bitcast.3, s32[1,16]{1,0:T(1,128)} %mask_hbm.1, f32[1]{0:T(128)S(6)} %copy.9.ell_s, f32[1]{0:T(128)S(6)} %copy.10.scl_s), custom_call_target="tpu_custom_call" | custom-call | tf_op jit(solution)/shard_map/ring_predict/pallas_call | solution.py:209
  59.1 0.7 %copy.8 = f32[2048,32]{0,1:T(8,128)} copy(f32[2048,32]{0,1:T(8,128)S(1)} %bitcast.2) | data formatting | bytes 524288

commit v4 on v3

--- a/solution.py
+++ b/solution.py
@@ -27,6 +27,7 @@
     vrows = r * half_rows // d
     spans = ((0, half_rows // 2), (half_rows // 2, half_rows // 4), (3 * half_rows // 4, half_rows // 4))
     n_piece = len(spans)
+    last = n_step - 1
 
     me = lax.axis_index("sp")
     chip, core = me // 2, me % 2
@@ -56,52 +57,47 @@
             src_ref=src_dst, dst_ref=src_dst, send_sem=send_sem, recv_sem=recv_sem,
             device_id={"sp": peer}, device_id_type=MESH)
 
-    def piece(j, half, q):
+    def piece(j, half, q, whole):
+        if whole:
+            return xs.at[j, half]
         lo, rows = spans[q]
         return xs.at[j, half, pl.ds(vrows + lo, rows) if q else pl.ds(0, vrows + rows)]
 
-    def to_right(s, q):
+    def to_right(s, q=0, whole=True):
         j = ((chip + n_chip - s // 2) % n_chip) * 2 + core
-        return remote(piece(j, s % 2, q), ring_send.at[0, s, q], ring_recv.at[0, s, q], right)
-
-    def to_left(s, q):
+        return remote(piece(j, s % 2, q, whole), ring_send.at[0, s, q], ring_recv.at[0, s, q], right)
+
+    def to_left(s, q=0, whole=True):
         j = ((chip + s // 2) % n_chip) * 2 + core
-        return remote(piece(j, 1 - s % 2, q), ring_send.at[1, s, q], ring_recv.at[1, s, q], left)
+        return remote(piece(j, 1 - s % 2, q, whole), ring_send.at[1, s, q], ring_recv.at[1, s, q], left)
 
     def source(u, c):
         h = u // 2 + 1
         return (((chip + n_chip - h) % n_chip) * 2 + c, u % 2), (((chip + h) % n_chip) * 2 + c, 1 - u % 2)
 
-    def from_ring(u, q):
+    def from_ring(u, q=0, whole=True):
         a, b = source(u, core)
-        return (remote(piece(*a, q), ring_send.at[0, u, q], ring_recv.at[0, u, q], left),
-                remote(piece(*b, q), ring_send.at[1, u, q], ring_recv.at[1, u, q], right))
-
-    def sibling(u, q, c):
+        return (remote(piece(*a, q, whole), ring_send.at[0, u, q], ring_recv.at[0, u, q], left),
+                remote(piece(*b, q, whole), ring_send.at[1, u, q], ring_recv.at[1, u, q], right))
+
+    def sibling(u, c, q=0, whole=True):
         a, b = source(u, c)
-        return (remote(piece(*a, q), sib_send.at[0, u, q], sib_recv.at[0, u, q], sib),
-                remote(piece(*b, q), sib_send.at[1, u, q], sib_recv.at[1, u, q], sib))
+        return (remote(piece(*a, q, whole), sib_send.at[0, u, q], sib_recv.at[0, u, q], sib),
+                remote(piece(*b, q, whole), sib_send.at[1, u, q], sib_recv.at[1, u, q], sib))
 
     def own(j, half):
         return remote(xs.at[j, half], own_send.at[half], own_recv.at[half], sib)
 
-    def ring_sent(s):
-        for q in range(n_piece):
-            for k in range(2):
-                remote(piece(0, 0, q), ring_send.at[k, s, q], ring_recv.at[k, s, q], right).wait_send()
-
-    def sibling_sent(u, qs):
-        for q in qs:
-            for k in range(2):
-                remote(piece(0, 0, q), sib_send.at[k, u, q], sib_recv.at[k, u, q], sib).wait_send()
+    def sent(sems, u, q=0, whole=True):
+        for k in range(2):
+            remote(piece(0, 0, q, whole), sems.at[k, u, q], ring_recv.at[k, u, q], sib).wait_send()
 
     for load in loads[:n_own]:
         load.wait()
     pl.semaphore_wait(barrier, 3)
     for s in range(2):
-        for q in range(n_piece):
-            to_right(s, q).start()
-            to_left(s, q).start()
+        to_right(s).start()
+        to_left(s).start()
     for half in range(2):
         own(me, half).start()
 
@@ -155,45 +151,63 @@
         own(sib, half).wait_recv()
         use_half(sib, half)
 
-    def arrive(u, q, forward):
-        ring = from_ring(u, q)
-        to_sib = sibling(u, q, core)
+    @pl.loop(0, last)
+    def _(u):
+        ring, to_sib = from_ring(u), sibling(u, core)
+        for k in range(2):
+            onward = (to_right, to_left)[k]
+            ring[k].wait_recv()
+
+            @pl.when(u < last - 2)
+            def _():
+                onward(u + 2).start()
+
+            @pl.when(u == last - 2)
+            def _():
+                for q in range(n_piece):
+                    onward(last, q, False).start()
+
+            to_sib[k].start()
+        for j, half in source(u, core):
+            use_half(j, half)
+        for copy in sibling(u, 1 - core):
+            copy.wait_recv()
+        for j, half in source(u, 1 - core):
+            use_half(j, half)
+
+        @pl.when(u > 0)
+        def _():
+            sent(ring_send, u - 1)
+            sent(sib_send, u - 1)
+
+    sent(ring_send, last - 1)
+    sent(sib_send, last - 1)
+    for half in range(2):
+        own(me, half).wait_send()
+
+    def arrive(q):
+        ring, to_sib = from_ring(last, q, False), sibling(last, core, q, False)
         for k in range(2):
             ring[k].wait_recv()
-            if forward:
-                @pl.when(u < n_step - 2)
-                def _():
-                    (to_right, to_left)[k](u + 2, q).start()
-
             to_sib[k].start()
 
-    def step(u, groups, forward):
-        for qs in groups:
-            for q in qs:
-                arrive(u, q, forward)
-            lo, rows = spans[qs[0]][0], sum(spans[q][1] for q in qs)
-            use_pair(u, core, lo, rows)
-            for q in qs:
-                for copy in sibling(u, q, 1 - core):
-                    copy.wait_recv()
-            use_pair(u, 1 - core, lo, rows)
-
-    @pl.loop(0, n_step - 1)
-    def _(u):
-        step(u, ((0,), (1, 2)), True)
-
-        @pl.when(u > 0)
-        def _():
-            ring_sent(u - 1)
-            sibling_sent(u - 1, range(n_piece))
-
-    ring_sent(n_step - 2)
-    sibling_sent(n_step - 2, range(n_piece))
-    for half in range(2):
-        own(me, half).wait_send()
-    step(n_step - 1, ((0,), (1,), (2,)), False)
-    ring_sent(n_step - 1)
-    sibling_sent(n_step - 1, range(n_piece))
+    def use_sibling(q):
+        for copy in sibling(last, 1 - core, q, False):
+            copy.wait_recv()
+        use_pair(last, 1 - core, *spans[q])
+
+    arrive(0)
+    use_pair(last, core, *spans[0])
+    use_sibling(0)
+    for q in range(1, n_piece):
+        arrive(q)
+        if q > 1:
+            use_sibling(q - 1)
+        use_pair(last, core, *spans[q])
+    use_sibling(n_piece - 1)
+    for q in range(n_piece):
+        sent(ring_send, last, q, False)
+        sent(sib_send, last, q, False)
 
 
 def solution(mesh):

time: 59.9 us -> 60.2 us (level)
  no operation moved by 1% of the time
where the time goes in v4:
time: 60.2 us; the launch traced here: 60.1 us
  Pallas kernels  58.1 us (97%)
  between operations  1.3 us (2%)
  local copies, waits for them, and re-layouts  0.71 us (1%)
    pallas_call x1, Pallas kernels, local_fn(): pl.pallas_call(functools.partial(kernel, n_dev), name='ring_predict', out...  58.1 us

profile of v4, /device:TPU:21, one launch (start us, length us, event | category | flops | bytes accessed | tf_op | source)
XLA Modules:
  0.0 60.1 jit_solution(1613494438916931079)
XLA Ops:
  1.3 58.1 %ring_predict.1 = f32[32,2048]{1,0:T(8,128)S(1)} custom-call(bf16[2048,512]{1,0:T(8,128)(2,1)} %z_hbm.1, bf16[512,512]{1,0:T(8,128)(2,1)} %x_hbm.1, bf16[32,512]{1,0:T(8,128)(2,1)} %bitcast.3, s32[1,16]{1,0:T(1,128)} %mask_hbm.1, f32[1]{0:T(128)S(6)} %copy.9.ell_s, f32[1]{0:T(128)S(6)} %copy.10.scl_s), custom_call_target="tpu_custom_call" | custom-call | tf_op jit(solution)/shard_map/ring_predict/pallas_call | solution.py:223
  59.4 0.7 %copy.8 = f32[2048,32]{0,1:T(8,128)} copy(f32[2048,32]{0,1:T(8,128)S(1)} %bitcast.2) | data formatting | bytes 524288

commit v5 on v4

--- a/solution.py
+++ b/solution.py
@@ -25,7 +25,7 @@
     r, nx = v_hbm.shape
     half_rows = nx // 2
     vrows = r * half_rows // d
-    spans = ((0, half_rows // 2), (half_rows // 2, half_rows // 4), (3 * half_rows // 4, half_rows // 4))
+    spans = ((0, half_rows // 2), (half_rows // 2, 5 * half_rows // 16), (13 * half_rows // 16, 3 * half_rows // 16))
     n_piece = len(spans)
     last = n_step - 1
 
@@ -134,22 +134,19 @@
             kern = (scale * jnp.exp2(half_dist * crow[0:1, :])).astype(BF16)
             y_ref[:, cols] += jnp.dot(vt_x, kern, preferred_element_type=F32)
 
-    def use_half(j, half):
-        accumulate(xs[j, half, vrows:vrows + half_rows, :], weighted(j, half, 0, half_rows))
+    def use_halves(*blocks):
+        x = jnp.concatenate([xs[j, half, vrows:vrows + half_rows, :] for j, half in blocks], axis=0)
+        accumulate(x, jnp.concatenate([weighted(j, half, 0, half_rows) for j, half in blocks], axis=1))
 
     def use_pair(u, c, lo, rows):
         a, b = source(u, c)
         x = jnp.concatenate([xs[a[0], a[1], pl.ds(vrows + lo, rows), :], xs[b[0], b[1], pl.ds(vrows + lo, rows), :]], axis=0)
         accumulate(x, jnp.concatenate([weighted(*a, lo, rows), weighted(*b, lo, rows)], axis=1))
 
-    @pl.loop(0, 2)
-    def _(half):
-        use_half(me, half)
-
-    @pl.loop(0, 2)
-    def _(half):
+    use_halves((me, 0), (me, 1))
+    for half in range(2):
         own(sib, half).wait_recv()
-        use_half(sib, half)
+    use_halves((sib, 0), (sib, 1))
 
     @pl.loop(0, last)
     def _(u):
@@ -168,12 +165,10 @@
                     onward(last, q, False).start()
 
             to_sib[k].start()
-        for j, half in source(u, core):
-            use_half(j, half)
+        use_halves(*source(u, core))
         for copy in sibling(u, 1 - core):
             copy.wait_recv()
-        for j, half in source(u, 1 - core):
-            use_half(j, half)
+        use_halves(*source(u, 1 - core))
 
         @pl.when(u > 0)
         def _():
@@ -233,14 +228,14 @@
                 pltpu.VMEM((8, mz), F32),
                 pltpu.VMEM((8, TILE), F32),
                 pltpu.SMEM((1, n_dev), jnp.int32),
-                pltpu.VMEM((nx // 2, LANES), F32),
+                pltpu.VMEM((nx, LANES), F32),
                 dma((8,)),
                 dma((2, n_step, 3)), dma((2, n_step, 3)),
                 dma((2, n_step, 3)), dma((2, n_step, 3)),
                 dma((2,)), dma((2,)),
             ],
             compiler_params=pltpu.CompilerParams(
-                collective_id=0, has_side_effects=True, vmem_limit_bytes=60 * 1024 * 1024),
+                collective_id=0, has_side_effects=True,  vmem_limit_bytes=60 * 1024 * 1024),
         )(z_rows, x_rows, v_rows.T, mask_row, length_scale, out_scale)
         return y_t.T
 

time: 60.2 us -> 60 us (level)
  no operation moved by 1% of the time
where the time goes in v5:
time: 60 us; the launch traced here: 59.9 us
  Pallas kernels  57.9 us (96%)
  between operations  1.3 us (2%)
  local copies, waits for them, and re-layouts  0.71 us (1%)
    pallas_call x1, Pallas kernels, local_fn(): pl.pallas_call(functools.partial(kernel, n_dev), name='ring_predict', out...  57.9 us

profile of v5, /device:TPU:21, one launch (start us, length us, event | category | flops | bytes accessed | tf_op | source)
XLA Modules:
  0.0 59.9 jit_solution(17386971205039407449)
XLA Ops:
  1.3 57.9 %ring_predict.1 = f32[32,2048]{1,0:T(8,128)S(1)} custom-call(bf16[2048,512]{1,0:T(8,128)(2,1)} %z_hbm.1, bf16[512,512]{1,0:T(8,128)(2,1)} %x_hbm.1, bf16[32,512]{1,0:T(8,128)(2,1)} %bitcast.3, s32[1,16]{1,0:T(1,128)} %mask_hbm.1, f32[1]{0:T(128)S(6)} %copy.9.ell_s, f32[1]{0:T(128)S(6)} %copy.10.scl_s), custom_call_target="tpu_custom_call" | custom-call | tf_op jit(solution)/shard_map/ring_predict/pallas_call | solution.py:218
  59.2 0.7 %copy.8 = f32[2048,32]{0,1:T(8,128)} copy(f32[2048,32]{0,1:T(8,128)S(1)} %bitcast.2) | data formatting | bytes 524288

commit v6 on v5

--- a/solution.py
+++ b/solution.py
@@ -170,16 +170,6 @@
             copy.wait_recv()
         use_halves(*source(u, 1 - core))
 
-        @pl.when(u > 0)
-        def _():
-            sent(ring_send, u - 1)
-            sent(sib_send, u - 1)
-
-    sent(ring_send, last - 1)
-    sent(sib_send, last - 1)
-    for half in range(2):
-        own(me, half).wait_send()
-
     def arrive(q):
         ring, to_sib = from_ring(last, q, False), sibling(last, core, q, False)
         for k in range(2):
@@ -200,6 +190,11 @@
             use_sibling(q - 1)
         use_pair(last, core, *spans[q])
     use_sibling(n_piece - 1)
+    for half in range(2):
+        own(me, half).wait_send()
+    for u in range(last):
+        sent(ring_send, u)
+        sent(sib_send, u)
     for q in range(n_piece):
         sent(ring_send, last, q, False)
         sent(sib_send, last, q, False)

time: 60 us -> 60 us (level)
  no operation moved by 1% of the time
where the time goes in v6:
time: 60 us; the launch traced here: 59.9 us
  Pallas kernels  57.9 us (96%)
  between operations  1.3 us (2%)
  local copies, waits for them, and re-layouts  0.71 us (1%)
    pallas_call x1, Pallas kernels, local_fn(): pl.pallas_call(functools.partial(kernel, n_dev), name='ring_predict', out...  57.9 us

profile of v6, /device:TPU:21, one launch (start us, length us, event | category | flops | bytes accessed | tf_op | source)
XLA Modules:
  0.0 59.9 jit_solution(15748341013357780663)
XLA Ops:
  1.3 57.9 %ring_predict.1 = f32[32,2048]{1,0:T(8,128)S(1)} custom-call(bf16[2048,512]{1,0:T(8,128)(2,1)} %z_hbm.1, bf16[512,512]{1,0:T(8,128)(2,1)} %x_hbm.1, bf16[32,512]{1,0:T(8,128)(2,1)} %bitcast.3, s32[1,16]{1,0:T(1,128)} %mask_hbm.1, f32[1]{0:T(128)S(6)} %copy.9.ell_s, f32[1]{0:T(128)S(6)} %copy.10.scl_s), custom_call_target="tpu_custom_call" | custom-call | tf_op jit(solution)/shard_map/ring_predict/pallas_call | solution.py:213
  59.2 0.7 %copy.8 = f32[2048,32]{0,1:T(8,128)} copy(f32[2048,32]{0,1:T(8,128)S(1)} %bitcast.2) | data formatting | bytes 524288

commit v7 on v3

--- a/solution.py
+++ b/solution.py
@@ -25,7 +25,7 @@
     r, nx = v_hbm.shape
     half_rows = nx // 2
     vrows = r * half_rows // d
-    spans = ((0, half_rows // 2), (half_rows // 2, half_rows // 4), (3 * half_rows // 4, half_rows // 4))
+    spans = ((0, half_rows // 2), (half_rows // 2, half_rows // 2))
     n_piece = len(spans)
 
     me = lax.axis_index("sp")
@@ -77,7 +77,7 @@
         return (remote(piece(*a, q), ring_send.at[0, u, q], ring_recv.at[0, u, q], left),
                 remote(piece(*b, q), ring_send.at[1, u, q], ring_recv.at[1, u, q], right))
 
-    def sibling(u, q, c):
+    def sibling(u, c, q):
         a, b = source(u, c)
         return (remote(piece(*a, q), sib_send.at[0, u, q], sib_recv.at[0, u, q], sib),
                 remote(piece(*b, q), sib_send.at[1, u, q], sib_recv.at[1, u, q], sib))
@@ -85,15 +85,9 @@
     def own(j, half):
         return remote(xs.at[j, half], own_send.at[half], own_recv.at[half], sib)
 
-    def ring_sent(s):
-        for q in range(n_piece):
-            for k in range(2):
-                remote(piece(0, 0, q), ring_send.at[k, s, q], ring_recv.at[k, s, q], right).wait_send()
-
-    def sibling_sent(u, qs):
-        for q in qs:
-            for k in range(2):
-                remote(piece(0, 0, q), sib_send.at[k, u, q], sib_recv.at[k, u, q], sib).wait_send()
+    def sent(sems, u, q):
+        for k in range(2):
+            remote(piece(0, 0, q), sems.at[k, u, q], ring_recv.at[k, u, q], sib).wait_send()
 
     for load in loads[:n_own]:
         load.wait()
@@ -138,62 +132,43 @@
             kern = (scale * jnp.exp2(half_dist * crow[0:1, :])).astype(BF16)
             y_ref[:, cols] += jnp.dot(vt_x, kern, preferred_element_type=F32)
 
-    def use_half(j, half):
-        accumulate(xs[j, half, vrows:vrows + half_rows, :], weighted(j, half, 0, half_rows))
+    def use_halves(*blocks):
+        x = jnp.concatenate([xs[j, half, vrows:vrows + half_rows, :] for j, half in blocks], axis=0)
+        accumulate(x, jnp.concatenate([weighted(j, half, 0, half_rows) for j, half in blocks], axis=1))
 
     def use_pair(u, c, lo, rows):
         a, b = source(u, c)
         x = jnp.concatenate([xs[a[0], a[1], pl.ds(vrows + lo, rows), :], xs[b[0], b[1], pl.ds(vrows + lo, rows), :]], axis=0)
         accumulate(x, jnp.concatenate([weighted(*a, lo, rows), weighted(*b, lo, rows)], axis=1))
 
-    @pl.loop(0, 2)
-    def _(half):
-        use_half(me, half)
-
-    @pl.loop(0, 2)
-    def _(half):
+    use_halves((me, 0), (me, 1))
+    for half in range(2):
         own(sib, half).wait_recv()
-        use_half(sib, half)
-
-    def arrive(u, q, forward):
-        ring = from_ring(u, q)
-        to_sib = sibling(u, q, core)
-        for k in range(2):
-            ring[k].wait_recv()
-            if forward:
+    use_halves((sib, 0), (sib, 1))
+
+    @pl.loop(0, n_step)
+    def _(u):
+        for q in range(n_piece):
+            ring, to_sib = from_ring(u, q), sibling(u, core, q)
+            for k in range(2):
+                ring[k].wait_recv()
+
                 @pl.when(u < n_step - 2)
                 def _():
                     (to_right, to_left)[k](u + 2, q).start()
 
-            to_sib[k].start()
-
-    def step(u, groups, forward):
-        for qs in groups:
-            for q in qs:
-                arrive(u, q, forward)
-            lo, rows = spans[qs[0]][0], sum(spans[q][1] for q in qs)
-            use_pair(u, core, lo, rows)
-            for q in qs:
-                for copy in sibling(u, q, 1 - core):
-                    copy.wait_recv()
-            use_pair(u, 1 - core, lo, rows)
-
-    @pl.loop(0, n_step - 1)
-    def _(u):
-        step(u, ((0,), (1, 2)), True)
-
-        @pl.when(u > 0)
-        def _():
-            ring_sent(u - 1)
-            sibling_sent(u - 1, range(n_piece))
-
-    ring_sent(n_step - 2)
-    sibling_sent(n_step - 2, range(n_piece))
+                to_sib[k].start()
+            use_pair(u, core, *spans[q])
+            for copy in sibling(u, 1 - core, q):
+                copy.wait_recv()
+            use_pair(u, 1 - core, *spans[q])
+
     for half in range(2):
         own(me, half).wait_send()
-    step(n_step - 1, ((0,), (1,), (2,)), False)
-    ring_sent(n_step - 1)
-    sibling_sent(n_step - 1, range(n_piece))
+    for u in range(n_step):
+        for q in range(n_piece):
+            sent(ring_send, u, q)
+            sent(sib_send, u, q)
 
 
 def solution(mesh):
@@ -219,14 +194,14 @@
                 pltpu.VMEM((8, mz), F32),
                 pltpu.VMEM((8, TILE), F32),
                 pltpu.SMEM((1, n_dev), jnp.int32),
-                pltpu.VMEM((nx // 2, LANES), F32),
+                pltpu.VMEM((nx, LANES), F32),
                 dma((8,)),
-                dma((2, n_step, 3)), dma((2, n_step, 3)),
-                dma((2, n_step, 3)), dma((2, n_step, 3)),
+                dma((2, n_step, 2)), dma((2, n_step, 2)),
+                dma((2, n_step, 2)), dma((2, n_step, 2)),
                 dma((2,)), dma((2,)),
             ],
             compiler_params=pltpu.CompilerParams(
-                collective_id=0, has_side_effects=True, vmem_limit_bytes=60 * 1024 * 1024),
+                collective_id=0, has_side_effects=True,  vmem_limit_bytes=60 * 1024 * 1024),
         )(z_rows, x_rows, v_rows.T, mask_row, length_scale, out_scale)
         return y_t.T
 

time: 59.9 us -> 57.9 us (0.967)
  Pallas kernels: 57.8 us -> 55.8 us
    pallas_call x1, Pallas kernels: 57.8 us -> 55.8 us  [local_fn(): pl.pallas_call(functools.partial(kernel, n_dev), name='ring_predict', out...]
where the time goes in v7:
time: 57.9 us; the launch traced here: 57.8 us
  Pallas kernels  55.8 us (96%)
  between operations  1.3 us (2%)
  local copies, waits for them, and re-layouts  0.71 us (1%)
    pallas_call x1, Pallas kernels, local_fn(): pl.pallas_call(functools.partial(kernel, n_dev), name='ring_predict', out...  55.8 us

profile of v7, /device:TPU:21, one launch (start us, length us, event | category | flops | bytes accessed | tf_op | source)
XLA Modules:
  0.0 57.8 jit_solution(16584379105476675681)
XLA Ops:
  1.3 55.8 %ring_predict.1 = f32[32,2048]{1,0:T(8,128)S(1)} custom-call(bf16[2048,512]{1,0:T(8,128)(2,1)} %z_hbm.1, bf16[512,512]{1,0:T(8,128)(2,1)} %x_hbm.1, bf16[32,512]{1,0:T(8,128)(2,1)} %bitcast.3, s32[1,16]{1,0:T(1,128)} %mask_hbm.1, f32[1]{0:T(128)S(6)} %copy.9.ell_s, f32[1]{0:T(128)S(6)} %copy.10.scl_s), custom_call_target="tpu_custom_call" | custom-call | tf_op jit(solution)/shard_map/ring_predict/pallas_call | solution.py:184
  57.1 0.7 %copy.8 = f32[2048,32]{0,1:T(8,128)} copy(f32[2048,32]{0,1:T(8,128)S(1)} %bitcast.2) | data formatting | bytes 524288

commit v8 on v5

--- a/solution.py
+++ b/solution.py
@@ -25,7 +25,7 @@
     r, nx = v_hbm.shape
     half_rows = nx // 2
     vrows = r * half_rows // d
-    spans = ((0, half_rows // 2), (half_rows // 2, 5 * half_rows // 16), (13 * half_rows // 16, 3 * half_rows // 16))
+    spans = ((0, half_rows // 2), (half_rows // 2, half_rows // 2))
     n_piece = len(spans)
     last = n_step - 1
 
@@ -191,15 +191,10 @@
             copy.wait_recv()
         use_pair(last, 1 - core, *spans[q])
 
-    arrive(0)
-    use_pair(last, core, *spans[0])
-    use_sibling(0)
-    for q in range(1, n_piece):
+    for q in range(n_piece):
         arrive(q)
-        if q > 1:
-            use_sibling(q - 1)
         use_pair(last, core, *spans[q])
-    use_sibling(n_piece - 1)
+        use_sibling(q)
     for q in range(n_piece):
         sent(ring_send, last, q, False)
         sent(sib_send, last, q, False)
@@ -230,8 +225,8 @@
                 pltpu.SMEM((1, n_dev), jnp.int32),
                 pltpu.VMEM((nx, LANES), F32),
                 dma((8,)),
-                dma((2, n_step, 3)), dma((2, n_step, 3)),
-                dma((2, n_step, 3)), dma((2, n_step, 3)),
+                dma((2, n_step, 2)), dma((2, n_step, 2)),
+                dma((2, n_step, 2)), dma((2, n_step, 2)),
                 dma((2,)), dma((2,)),
             ],
             compiler_params=pltpu.CompilerParams(

time: 60 us -> 58.6 us (0.977)
  Pallas kernels: 57.9 us -> 56.4 us
    pallas_call x1, Pallas kernels: 57.9 us -> 56.4 us  [local_fn(): pl.pallas_call(functools.partial(kernel, n_dev), name='ring_predict', out...]
where the time goes in v8:
time: 58.6 us; the launch traced here: 58.4 us
  Pallas kernels  56.4 us (96%)
  between operations  1.3 us (2%)
  local copies, waits for them, and re-layouts  0.71 us (1%)
    pallas_call x1, Pallas kernels, local_fn(): pl.pallas_call(functools.partial(kernel, n_dev), name='ring_predict', out...  56.4 us

profile of v8, /device:TPU:21, one launch (start us, length us, event | category | flops | bytes accessed | tf_op | source)
XLA Modules:
  0.0 58.4 jit_solution(13403754172015276723)
XLA Ops:
  1.3 56.4 %ring_predict.1 = f32[32,2048]{1,0:T(8,128)S(1)} custom-call(bf16[2048,512]{1,0:T(8,128)(2,1)} %z_hbm.1, bf16[512,512]{1,0:T(8,128)(2,1)} %x_hbm.1, bf16[32,512]{1,0:T(8,128)(2,1)} %bitcast.3, s32[1,16]{1,0:T(1,128)} %mask_hbm.1, f32[1]{0:T(128)S(6)} %copy.9.ell_s, f32[1]{0:T(128)S(6)} %copy.10.scl_s), custom_call_target="tpu_custom_call" | custom-call | tf_op jit(solution)/shard_map/ring_predict/pallas_call | solution.py:213
  57.7 0.7 %copy.8 = f32[2048,32]{0,1:T(8,128)} copy(f32[2048,32]{0,1:T(8,128)S(1)} %bitcast.2) | data formatting | bytes 524288
